TPU v7x, 32 devices: a whole 2x2x4 slice. The times are simulated.
32 devices in a mesh: gy: 8 (over z, x), gx: 4 (over y, core).
Axes of the slice: x: 2, y: 2, z: 4, core: 2. Of those that a mesh axis runs over, the one named last changes fastest.
Arguments:
- imbalance: float32 [4, 1024, 2048], P(None, 'gy', 'gx'), may hold values from -9 to 9
- flow: float32 [2, 4, 1024, 2048], P(None, None, 'gy', 'gx'), may hold values from -3 to 3
- potential: float32 [4, 1024, 2048], P(None, 'gy', 'gx'), may hold values from -5 to 5
- cost: float32 [1024, 2048], P('gy', 'gx'), may hold values from 0.2 to 2
Outputs:
- flow_out: float32 [2, 4, 1024, 2048], P(None, None, 'gy', 'gx')
- potential_out: float32 [4, 1024, 2048], P(None, 'gy', 'gx')
- residual: float32 [4], replicated
All inputs are finite; a program needn't handle non-finite values.
Results may differ from a plain program's by a relative error of at most 0.0001.
Values sent between devices are 32-bit elements; how exact they have to be, the bound alone decides.
A program may use at most 64 MiB of HBM per device.

v0:
```python
import jax
import jax.numpy as jnp
from jax import lax
from jax.sharding import PartitionSpec as P

ITERS = 12
initial_step = 0.35
epsilon = 1e-06


def shifted(value, axis, steps):
    count = lax.axis_size(axis)
    leading, last = (max(0, -steps), min(count, count - steps))
    return lax.ppermute(value, axis, [(source, source + steps) for source in range(leading, last)])


def gradient(potential):
    from_below = shifted(potential[:, 0, :], "gy", -1)
    from_right = shifted(potential[:, :, 0], "gx", -1)
    slope_down = jnp.concatenate([potential[:, 1:, :], from_below[:, None, :]], 1) - potential
    slope_right = jnp.concatenate([potential[:, :, 1:], from_right[:, :, None]], 2) - potential
    return (slope_down, slope_right)


def divergence(flow_down, flow_right):
    from_above = shifted(flow_down[:, -1, :], "gy", 1)
    from_left = shifted(flow_right[:, :, -1], "gx", 1)
    above_rows = jnp.concatenate([from_above[:, None, :], flow_down[:, :-1, :]], 1)
    left_cols = jnp.concatenate([from_left[:, :, None], flow_right[:, :, :-1]], 2)
    return flow_down - above_rows + flow_right - left_cols


def shrink(moved_down, moved_right, threshold):
    magnitude = jnp.sqrt(moved_down * moved_down + moved_right * moved_right)
    factor = jnp.maximum(magnitude - threshold, 0.0) / jnp.maximum(magnitude, threshold)
    return (factor * moved_down, factor * moved_right)


def local(imbalance, flow, potential, cost):
    local_rows, local_cols = cost.shape

    def primal(flow_down, flow_right, field, spread_old, primal_rate):
        slope_down, slope_right = gradient(field)
        rate_now = primal_rate[:, None, None]
        new_down, new_right = shrink(
            flow_down + rate_now * slope_down,
            flow_right + rate_now * slope_right,
            rate_now * cost[None],
        )
        return (new_down, new_right, spread_old, None)

    spread_start = divergence(flow[0], flow[1])

    def iterate(carried, with_stats):
        flow_down, flow_right, field, spread_old, primal_rate, dual_rate = carried
        new_down, new_right, spread_old, spread_new = primal(
            flow_down, flow_right, field, spread_old, primal_rate
        )
        if with_stats:
            diff_down = new_down - flow_down
            diff_right = new_right - flow_right
            primal_local = jnp.sum(diff_down * diff_down + diff_right * diff_right, axis=(1, 2))
        spread_new = divergence(new_down, new_right)
        new_field = field + dual_rate[:, None, None] * (2.0 * spread_new - spread_old - imbalance)
        if with_stats:
            change = new_field - field
            dual_local = jnp.sum(change * change, axis=(1, 2))
            primal_change, dual_change = lax.psum((primal_local, dual_local), ("gy", "gx"))
            rescale = jnp.sqrt(jnp.sqrt((primal_change + epsilon) / (dual_change + epsilon)))
            primal_rate = primal_rate / rescale
            dual_rate = dual_rate * rescale
        return (new_down, new_right, new_field, spread_new, primal_rate, dual_rate)

    def loop_turn(counter, carried):
        return iterate(carried, True)

    starting = jnp.full((potential.shape[0],), initial_step, jnp.float32)
    carried = (flow[0], flow[1], potential, spread_start, starting, starting)
    carried = lax.fori_loop(0, ITERS - 1, loop_turn, carried)
    closing = iterate(carried, False)
    shortfall = closing[3] - imbalance
    total_sum = lax.psum(jnp.sum(shortfall * shortfall, axis=(1, 2)), ("gy", "gx"))
    cell_count = local_rows * lax.axis_size("gy") * local_cols * lax.axis_size("gx")
    residual = total_sum / cell_count
    return (jnp.stack([closing[0], closing[1]]), closing[2], residual)


def solution(mesh):
    placed = (P(None, "gy", "gx"), P(None, None, "gy", "gx"), P(None, "gy", "gx"), P("gy", "gx"))
    return jax.shard_map(
        local,
        mesh=mesh,
        in_specs=placed,
        out_specs=(P(None, None, "gy", "gx"), P(None, "gy", "gx"), P()),
        check_vma=False,
    )
```

profile of v0, /device:TPU:0, one launch (start us, length us, event | category | flops | bytes accessed | tf_op | source)
XLA Modules:
  0.0 887.7 jit_solution(16072063486011655081)
XLA Ops:
  3.7 4.9 collective-permute-start.4
  21.5 791.1 %while.21 = (s32[]{:T(128)}, f32[4,128,512]{1,0,2:T(4,128)S(1)}, f32[4,128,512]{1,0,2:T(4,128)S(1)}, f32[4,128,512]{1,0,2:T(4,128)S(1)}, f32[4,128,512]{1,0,2:T(...) while((s32[]{:T(128)}, f32[4,128,512]{1,0,2:T(4,128)S(1)}, ...), condition=%wide.region_5.0_spmd.clone, body=%wide.region_0.0_spmd.clone.sunk | while | flops 10747943 | bytes 36053636 | solution.py:79
  48.4 5.4 multiply_reduce_fusion.3
  53.8 42.1 %all-reduce.2 = (f32[4]{0:T(128)S(1)}, f32[4]{0:T(128)S(1)}) all-reduce(f32[4]{0:T(128)S(1)} %get-tuple-element.228, f32[4]{0:T(128)S(1)} %get-tuple-element.229), channel_id=1, replica_groups=mesh['gy'=8,'gx'=4] {'gy','gx'}, use_global_device_ids=true, to_apply=%region_4.0 | all-reduce | flops 8 | bytes 64 | tf_op jit(solution)/shard_map/while/body/eval_jaxpr/psum | solution.py:68
  122.2 5.4 multiply_reduce_fusion.3
  127.5 39.6 %all-reduce.2 = (f32[4]{0:T(128)S(1)}, f32[4]{0:T(128)S(1)}) all-reduce(f32[4]{0:T(128)S(1)} %get-tuple-element.228, f32[4]{0:T(128)S(1)} %get-tuple-element.229), channel_id=1, replica_groups=mesh['gy'=8,'gx'=4] {'gy','gx'}, use_global_device_ids=true, to_apply=%region_4.0 | all-reduce | flops 8 | bytes 64 | tf_op jit(solution)/shard_map/while/body/eval_jaxpr/psum | solution.py:68
  184.4 4.8 collective-permute-start.3
  193.4 5.4 multiply_reduce_fusion.3
  198.8 40.4 %all-reduce.2 = (f32[4]{0:T(128)S(1)}, f32[4]{0:T(128)S(1)}) all-reduce(f32[4]{0:T(128)S(1)} %get-tuple-element.228, f32[4]{0:T(128)S(1)} %get-tuple-element.229), channel_id=1, replica_groups=mesh['gy'=8,'gx'=4] {'gy','gx'}, use_global_device_ids=true, to_apply=%region_4.0 | all-reduce | flops 8 | bytes 64 | tf_op jit(solution)/shard_map/while/body/eval_jaxpr/psum | solution.py:68
  256.4 4.8 collective-permute-start.3
  265.5 5.4 multiply_reduce_fusion.3
  270.9 39.6 %all-reduce.2 = (f32[4]{0:T(128)S(1)}, f32[4]{0:T(128)S(1)}) all-reduce(f32[4]{0:T(128)S(1)} %get-tuple-element.228, f32[4]{0:T(128)S(1)} %get-tuple-element.229), channel_id=1, replica_groups=mesh['gy'=8,'gx'=4] {'gy','gx'}, use_global_device_ids=true, to_apply=%region_4.0 | all-reduce | flops 8 | bytes 64 | tf_op jit(solution)/shard_map/while/body/eval_jaxpr/psum | solution.py:68
  327.7 4.8 collective-permute-start.3
  336.7 5.4 multiply_reduce_fusion.3
  342.1 40.4 %all-reduce.2 = (f32[4]{0:T(128)S(1)}, f32[4]{0:T(128)S(1)}) all-reduce(f32[4]{0:T(128)S(1)} %get-tuple-element.228, f32[4]{0:T(128)S(1)} %get-tuple-element.229), channel_id=1, replica_groups=mesh['gy'=8,'gx'=4] {'gy','gx'}, use_global_device_ids=true, to_apply=%region_4.0 | all-reduce | flops 8 | bytes 64 | tf_op jit(solution)/shard_map/while/body/eval_jaxpr/psum | solution.py:68
  399.8 4.8 collective-permute-start.3
  408.8 5.4 multiply_reduce_fusion.3
  414.2 39.6 %all-reduce.2 = (f32[4]{0:T(128)S(1)}, f32[4]{0:T(128)S(1)}) all-reduce(f32[4]{0:T(128)S(1)} %get-tuple-element.228, f32[4]{0:T(128)S(1)} %get-tuple-element.229), channel_id=1, replica_groups=mesh['gy'=8,'gx'=4] {'gy','gx'}, use_global_device_ids=true, to_apply=%region_4.0 | all-reduce | flops 8 | bytes 64 | tf_op jit(solution)/shard_map/while/body/eval_jaxpr/psum | solution.py:68
  480.1 5.4 multiply_reduce_fusion.3
  485.5 40.4 %all-reduce.2 = (f32[4]{0:T(128)S(1)}, f32[4]{0:T(128)S(1)}) all-reduce(f32[4]{0:T(128)S(1)} %get-tuple-element.228, f32[4]{0:T(128)S(1)} %get-tuple-element.229), channel_id=1, replica_groups=mesh['gy'=8,'gx'=4] {'gy','gx'}, use_global_device_ids=true, to_apply=%region_4.0 | all-reduce | flops 8 | bytes 64 | tf_op jit(solution)/shard_map/while/body/eval_jaxpr/psum | solution.py:68
  552.1 5.4 multiply_reduce_fusion.3
  557.5 39.6 %all-reduce.2 = (f32[4]{0:T(128)S(1)}, f32[4]{0:T(128)S(1)}) all-reduce(f32[4]{0:T(128)S(1)} %get-tuple-element.228, f32[4]{0:T(128)S(1)} %get-tuple-element.229), channel_id=1, replica_groups=mesh['gy'=8,'gx'=4] {'gy','gx'}, use_global_device_ids=true, to_apply=%region_4.0 | all-reduce | flops 8 | bytes 64 | tf_op jit(solution)/shard_map/while/body/eval_jaxpr/psum | solution.py:68
  614.3 4.8 collective-permute-start.3
  623.4 5.4 multiply_reduce_fusion.3
  628.8 40.4 %all-reduce.2 = (f32[4]{0:T(128)S(1)}, f32[4]{0:T(128)S(1)}) all-reduce(f32[4]{0:T(128)S(1)} %get-tuple-element.228, f32[4]{0:T(128)S(1)} %get-tuple-element.229), channel_id=1, replica_groups=mesh['gy'=8,'gx'=4] {'gy','gx'}, use_global_device_ids=true, to_apply=%region_4.0 | all-reduce | flops 8 | bytes 64 | tf_op jit(solution)/shard_map/while/body/eval_jaxpr/psum | solution.py:68
  686.4 4.8 collective-permute-start.3
  695.5 5.4 multiply_reduce_fusion.3
  700.9 39.6 %all-reduce.2 = (f32[4]{0:T(128)S(1)}, f32[4]{0:T(128)S(1)}) all-reduce(f32[4]{0:T(128)S(1)} %get-tuple-element.228, f32[4]{0:T(128)S(1)} %get-tuple-element.229), channel_id=1, replica_groups=mesh['gy'=8,'gx'=4] {'gy','gx'}, use_global_device_ids=true, to_apply=%region_4.0 | all-reduce | flops 8 | bytes 64 | tf_op jit(solution)/shard_map/while/body/eval_jaxpr/psum | solution.py:68
  757.7 4.8 collective-permute-start.3
  766.7 5.4 multiply_reduce_fusion.3
  772.1 40.4 %all-reduce.2 = (f32[4]{0:T(128)S(1)}, f32[4]{0:T(128)S(1)}) all-reduce(f32[4]{0:T(128)S(1)} %get-tuple-element.228, f32[4]{0:T(128)S(1)} %get-tuple-element.229), channel_id=1, replica_groups=mesh['gy'=8,'gx'=4] {'gy','gx'}, use_global_device_ids=true, to_apply=%region_4.0 | all-reduce | flops 8 | bytes 64 | tf_op jit(solution)/shard_map/while/body/eval_jaxpr/psum | solution.py:68
  841.9 42.0 %psum.21 = f32[4]{0:T(128)S(1)} all-reduce(f32[4]{0:T(128)S(1)} %get-tuple-element.148), channel_id=1, replica_groups=mesh['gy'=8,'gx'=4] {'gy','gx'}, use_global_device_ids=true, to_apply=%region_7.0 | all-reduce | flops 4 | bytes 32 | tf_op jit(solution)/shard_map/psum | solution.py:82
  (335 shorter events, 303.3 us)
Async XLA Ops:
  3.7 13.1 %collective-permute-start.4 = (f32[4,512]{1,0:T(4,128)S(1)}, f32[4,512]{1,0:T(4,128)S(1)}, u32[]{:S(2)}, u32[]{:S(2)}) collective-permute-start(f32[4,512]{1,0:T(4,128)S(1)} %bitcast.78), channel_id=1, source_target_pairs={{0,4},{4,8},{8,12},{12,16},{16,20},{20,24},{24,28},{1,5},{5,9},{9,... | collective-permute-start | bytes 24584 | tf_op jit(solution)/shard_map/ppermute | solution.py:14
  9.0 9.1 %collective-permute-start.5 = (f32[4,128]{1,0:T(4,128)S(1)}, f32[4,128]{1,0:T(4,128)S(1)}, u32[]{:S(2)}, u32[]{:S(2)}) collective-permute-start(f32[4,128]{1,0:T(4,128)S(1)} %slice_bitcast_fusion.2), channel_id=1, source_target_pairs={{0,1},{1,2},{2,3},{4,5},{5,6},{6,7},{8,9},{9,10},{10,11},{12,13},{... | collective-permute-start | bytes 6152 | tf_op jit(solution)/shard_map/ppermute | solution.py:14
  21.5 8.5 collective-permute-start
  38.4 8.7 collective-permute-start.3
  96.0 8.8 collective-permute-start
  97.6 5.8 collective-permute-start.1
  113.1 7.7 collective-permute-start.3
  167.2 8.8 collective-permute-start
  168.9 5.8 collective-permute-start.1
  184.4 7.7 collective-permute-start.3
  239.3 8.8 collective-permute-start
  241.0 5.8 collective-permute-start.1
  256.4 7.7 collective-permute-start.3
  310.6 8.8 collective-permute-start
  312.2 5.8 collective-permute-start.1
  327.7 7.7 collective-permute-start.3
  382.6 8.8 collective-permute-start
  399.8 7.7 collective-permute-start.3
  453.9 8.8 collective-permute-start
  471.0 7.7 collective-permute-start.3
  526.0 8.8 collective-permute-start
  543.1 7.7 collective-permute-start.3
  597.2 8.8 collective-permute-start
  614.3 7.7 collective-permute-start.3
  669.3 8.8 collective-permute-start
  686.4 7.7 collective-permute-start.3
  740.5 8.8 collective-permute-start
  757.7 7.7 collective-permute-start.3
  813.0 12.8 %collective-permute-start.6 = (f32[4,512]{1,0:T(4,128)S(1)}, f32[4,512]{1,0:T(4,128)S(1)}, u32[]{:S(2)}, u32[]{:S(2)}) collective-permute-start(f32[4,512]{1,0:T(4,128)S(1)} %bitcast.77), channel_id=1, source_target_pairs={{4,0},{8,4},{12,8},{16,12},{20,16},{24,20},{28,24},{5,1},{9,5},{13... | collective-permute-start | bytes 24584 | tf_op jit(solution)/shard_map/ppermute | solution.py:14
  814.3 10.7 %collective-permute-start.7 = (f32[4,128]{1,0:T(4,128)S(1)}, f32[4,128]{1,0:T(4,128)S(1)}, u32[]{:S(2)}, u32[]{:S(2)}) collective-permute-start(f32[4,128]{1,0:T(4,128)S(1)} %slice_bitcast_fusion.3), channel_id=1, source_target_pairs={{1,0},{2,1},{3,2},{5,4},{6,5},{7,6},{9,8},{10,9},{11,10},{13,12},{... | collective-permute-start | bytes 6152 | tf_op jit(solution)/shard_map/ppermute | solution.py:14
  829.6 9.4 %collective-permute-start.9 = (f32[4,128]{1,0:T(4,128)S(1)}, f32[4,128]{1,0:T(4,128)S(1)}, u32[]{:S(2)}, u32[]{:S(2)}) collective-permute-start(f32[4,128]{1,0:T(4,128)S(1)} %slice_reduce_fusion), channel_id=1, source_target_pairs={{0,1},{1,2},{2,3},{4,5},{5,6},{6,7},{8,9},{9,10},{10,11},{12,13},{... | collective-permute-start | bytes 6152 | tf_op jit(solution)/shard_map/ppermute | solution.py:14
  832.6 6.5 collective-permute-start.8
  (34 other events, 145.1 us)
where the time goes:
time: 891 us; the launch traced here: 888 us
  blocking collectives  484 us (54%)
  local copies, waits for them, and re-layouts  132 us (15%)
  other arithmetic  131 us (15%)
  starting transfers between devices  118 us (13%)
  waiting for transfers between devices  19.6 us (2%)
    psum x11, blocking collectives, iterate(): lax.psum((primal_local, dual_local), ('gy', 'gx'))  442 us
    ppermute x50, starting transfers between devices, shifted(): lax.ppermute(value, axis, [(source, source + steps) for source in range(l...  118 us
    reduce_sum x11, other arithmetic, iterate(): dual_local = jnp.sum(change * change, axis=(1, 2))  59.3 us
    div x11, other arithmetic, shrink(): jnp.maximum(magnitude - threshold, 0.0) / jnp.maximum(magnitude, threshold)  42.2 us
    psum x1, blocking collectives, local(): lax.psum(jnp.sum(shortfall * shortfall, axis=(1, 2)), ('gy', 'gx'))  42 us
    slice x25, local copies, waits for them, and re-layouts, divergence(): from_above = shifted(flow_down[:, -1, :], 'gy', 1)  35.4 us
    slice x12, local copies, waits for them, and re-layouts, gradient(): potential[:, 1:, :]  20.5 us
    ppermute x50, waiting for transfers between devices, shifted(): lax.ppermute(value, axis, [(source, source + steps) for source in range(l...  19.6 us
  transfers between devices with their start and end apart: 50, of which 11 were waited for; matrix products, arithmetic and copies ran while one was open for 11% of the time, Pallas kernels for 0%

commit v1 on v0

--- a/solution.py
+++ b/solution.py
@@ -65,7 +65,7 @@
         if with_stats:
             change = new_field - field
             dual_local = jnp.sum(change * change, axis=(1, 2))
-            primal_change, dual_change = lax.psum((primal_local, dual_local), ("gy", "gx"))
+            primal_change, dual_change = lax.psum(lax.psum((primal_local, dual_local), "gx"), "gy")
             rescale = jnp.sqrt(jnp.sqrt((primal_change + epsilon) / (dual_change + epsilon)))
             primal_rate = primal_rate / rescale
             dual_rate = dual_rate * rescale

time: 891 us -> 724 us (0.81)
  blocking collectives: 484 us -> 332 us
  starting transfers between devices: 118 us -> 107 us
    psum x11 -> x22, blocking collectives: 442 us -> 291 us  [the longest x11 201 us: iterate(): lax.psum(lax.psum((primal_local, dual_local), 'gx'), 'gy')]
    ppermute x50, starting transfers between devices: 118 us -> 107 us  [shifted(): lax.ppermute(value, axis, [(source, source + steps) for source in range(l...]
  transfers between devices with their start and end apart: 50 -> 50, of which waited for: 11 -> 11; matrix products, arithmetic and copies ran while one was open for 11% -> 13% of each run, Pallas kernels for 0% -> 0%
where the time goes in v1:
time: 724 us; the launch traced here: 721 us
  blocking collectives  332 us (46%)
  local copies, waits for them, and re-layouts  132 us (18%)
  other arithmetic  132 us (18%)
  starting transfers between devices  107 us (15%)
  waiting for transfers between devices  17 us (2%)
    psum x11, blocking collectives, iterate(): lax.psum(lax.psum((primal_local, dual_local), 'gx'), 'gy')  201 us
    ppermute x50, starting transfers between devices, shifted(): lax.ppermute(value, axis, [(source, source + steps) for source in range(l...  107 us
    psum x11, blocking collectives, iterate(): lax.psum((primal_local, dual_local), 'gx')  90.1 us
    reduce_sum x11, other arithmetic, iterate(): dual_local = jnp.sum(change * change, axis=(1, 2))  59.3 us
    div x11, other arithmetic, shrink(): jnp.maximum(magnitude - threshold, 0.0) / jnp.maximum(magnitude, threshold)  42.2 us
    psum x1, blocking collectives, local(): lax.psum(jnp.sum(shortfall * shortfall, axis=(1, 2)), ('gy', 'gx'))  40.7 us
    slice x25, local copies, waits for them, and re-layouts, divergence(): from_above = shifted(flow_down[:, -1, :], 'gy', 1)  35.4 us
    slice x12, local copies, waits for them, and re-layouts, gradient(): potential[:, 1:, :]  20.4 us
  transfers between devices with their start and end apart: 50, of which 11 were waited for; matrix products, arithmetic and copies ran while one was open for 13% of the time, Pallas kernels for 0%

profile of v1, /device:TPU:0, one launch (start us, length us, event | category | flops | bytes accessed | tf_op | source)
XLA Modules:
  0.0 721.4 jit_solution(14662905804608947074)
XLA Ops:
  21.6 626.1 %while.21 = (s32[]{:T(128)}, f32[4,128,512]{1,0,2:T(4,128)S(1)}, f32[4,128,512]{1,0,2:T(4,128)S(1)}, f32[4,128,512]{1,0,2:T(4,128)S(1)}, f32[4,128,512]{1,0,2:T(...) while((s32[]{:T(128)}, f32[4,128,512]{1,0,2:T(4,128)S(1)}, ...), condition=%wide.region_7.0_spmd.clone, body=%wide.region_0.0_spmd.clone.sunk | while | flops 10747951 | bytes 36053700 | solution.py:79
  48.5 5.4 multiply_reduce_fusion.3
  53.9 9.0 %all-reduce.4 = (f32[4]{0:T(128)S(1)}, f32[4]{0:T(128)S(1)}) all-reduce(f32[4]{0:T(128)S(1)} %get-tuple-element.232, f32[4]{0:T(128)S(1)} %get-tuple-element.233), channel_id=1, replica_groups=mesh['gy'=8,'gx'=4] {'gx'}, use_global_device_ids=true, to_apply=%region_5.0 | all-reduce | flops 8 | bytes 64 | tf_op jit(solution)/shard_map/while/body/eval_jaxpr/psum | solution.py:68
  62.9 18.5 %all-reduce.5 = (f32[4]{0:T(128)S(1)}, f32[4]{0:T(128)S(1)}) all-reduce(f32[4]{0:T(128)S(1)} %get-tuple-element.234, f32[4]{0:T(128)S(1)} %get-tuple-element.235), channel_id=1, replica_groups=mesh['gy'=8,'gx'=4] {'gy'}, use_global_device_ids=true, to_apply=%region_6.0 | all-reduce | flops 8 | bytes 64 | tf_op jit(solution)/shard_map/while/body/eval_jaxpr/psum | solution.py:68
  106.2 5.4 multiply_reduce_fusion.3
  111.6 7.9 %all-reduce.4 = (f32[4]{0:T(128)S(1)}, f32[4]{0:T(128)S(1)}) all-reduce(f32[4]{0:T(128)S(1)} %get-tuple-element.232, f32[4]{0:T(128)S(1)} %get-tuple-element.233), channel_id=1, replica_groups=mesh['gy'=8,'gx'=4] {'gx'}, use_global_device_ids=true, to_apply=%region_5.0 | all-reduce | flops 8 | bytes 64 | tf_op jit(solution)/shard_map/while/body/eval_jaxpr/psum | solution.py:68
  119.5 18.2 %all-reduce.5 = (f32[4]{0:T(128)S(1)}, f32[4]{0:T(128)S(1)}) all-reduce(f32[4]{0:T(128)S(1)} %get-tuple-element.234, f32[4]{0:T(128)S(1)} %get-tuple-element.235), channel_id=1, replica_groups=mesh['gy'=8,'gx'=4] {'gy'}, use_global_device_ids=true, to_apply=%region_6.0 | all-reduce | flops 8 | bytes 64 | tf_op jit(solution)/shard_map/while/body/eval_jaxpr/psum | solution.py:68
  162.7 5.4 multiply_reduce_fusion.3
  168.0 8.1 %all-reduce.4 = (f32[4]{0:T(128)S(1)}, f32[4]{0:T(128)S(1)}) all-reduce(f32[4]{0:T(128)S(1)} %get-tuple-element.232, f32[4]{0:T(128)S(1)} %get-tuple-element.233), channel_id=1, replica_groups=mesh['gy'=8,'gx'=4] {'gx'}, use_global_device_ids=true, to_apply=%region_5.0 | all-reduce | flops 8 | bytes 64 | tf_op jit(solution)/shard_map/while/body/eval_jaxpr/psum | solution.py:68
  176.2 18.2 %all-reduce.5 = (f32[4]{0:T(128)S(1)}, f32[4]{0:T(128)S(1)}) all-reduce(f32[4]{0:T(128)S(1)} %get-tuple-element.234, f32[4]{0:T(128)S(1)} %get-tuple-element.235), channel_id=1, replica_groups=mesh['gy'=8,'gx'=4] {'gy'}, use_global_device_ids=true, to_apply=%region_6.0 | all-reduce | flops 8 | bytes 64 | tf_op jit(solution)/shard_map/while/body/eval_jaxpr/psum | solution.py:68
  219.3 5.4 multiply_reduce_fusion.3
  224.7 8.1 %all-reduce.4 = (f32[4]{0:T(128)S(1)}, f32[4]{0:T(128)S(1)}) all-reduce(f32[4]{0:T(128)S(1)} %get-tuple-element.232, f32[4]{0:T(128)S(1)} %get-tuple-element.233), channel_id=1, replica_groups=mesh['gy'=8,'gx'=4] {'gx'}, use_global_device_ids=true, to_apply=%region_5.0 | all-reduce | flops 8 | bytes 64 | tf_op jit(solution)/shard_map/while/body/eval_jaxpr/psum | solution.py:68
  232.8 18.2 %all-reduce.5 = (f32[4]{0:T(128)S(1)}, f32[4]{0:T(128)S(1)}) all-reduce(f32[4]{0:T(128)S(1)} %get-tuple-element.234, f32[4]{0:T(128)S(1)} %get-tuple-element.235), channel_id=1, replica_groups=mesh['gy'=8,'gx'=4] {'gy'}, use_global_device_ids=true, to_apply=%region_6.0 | all-reduce | flops 8 | bytes 64 | tf_op jit(solution)/shard_map/while/body/eval_jaxpr/psum | solution.py:68
  276.0 5.4 multiply_reduce_fusion.3
  281.4 8.1 %all-reduce.4 = (f32[4]{0:T(128)S(1)}, f32[4]{0:T(128)S(1)}) all-reduce(f32[4]{0:T(128)S(1)} %get-tuple-element.232, f32[4]{0:T(128)S(1)} %get-tuple-element.233), channel_id=1, replica_groups=mesh['gy'=8,'gx'=4] {'gx'}, use_global_device_ids=true, to_apply=%region_5.0 | all-reduce | flops 8 | bytes 64 | tf_op jit(solution)/shard_map/while/body/eval_jaxpr/psum | solution.py:68
  289.5 18.2 %all-reduce.5 = (f32[4]{0:T(128)S(1)}, f32[4]{0:T(128)S(1)}) all-reduce(f32[4]{0:T(128)S(1)} %get-tuple-element.234, f32[4]{0:T(128)S(1)} %get-tuple-element.235), channel_id=1, replica_groups=mesh['gy'=8,'gx'=4] {'gy'}, use_global_device_ids=true, to_apply=%region_6.0 | all-reduce | flops 8 | bytes 64 | tf_op jit(solution)/shard_map/while/body/eval_jaxpr/psum | solution.py:68
  332.6 5.4 multiply_reduce_fusion.3
  338.0 8.1 %all-reduce.4 = (f32[4]{0:T(128)S(1)}, f32[4]{0:T(128)S(1)}) all-reduce(f32[4]{0:T(128)S(1)} %get-tuple-element.232, f32[4]{0:T(128)S(1)} %get-tuple-element.233), channel_id=1, replica_groups=mesh['gy'=8,'gx'=4] {'gx'}, use_global_device_ids=true, to_apply=%region_5.0 | all-reduce | flops 8 | bytes 64 | tf_op jit(solution)/shard_map/while/body/eval_jaxpr/psum | solution.py:68
  346.2 18.2 %all-reduce.5 = (f32[4]{0:T(128)S(1)}, f32[4]{0:T(128)S(1)}) all-reduce(f32[4]{0:T(128)S(1)} %get-tuple-element.234, f32[4]{0:T(128)S(1)} %get-tuple-element.235), channel_id=1, replica_groups=mesh['gy'=8,'gx'=4] {'gy'}, use_global_device_ids=true, to_apply=%region_6.0 | all-reduce | flops 8 | bytes 64 | tf_op jit(solution)/shard_map/while/body/eval_jaxpr/psum | solution.py:68
  389.3 5.4 multiply_reduce_fusion.3
  394.7 8.1 %all-reduce.4 = (f32[4]{0:T(128)S(1)}, f32[4]{0:T(128)S(1)}) all-reduce(f32[4]{0:T(128)S(1)} %get-tuple-element.232, f32[4]{0:T(128)S(1)} %get-tuple-element.233), channel_id=1, replica_groups=mesh['gy'=8,'gx'=4] {'gx'}, use_global_device_ids=true, to_apply=%region_5.0 | all-reduce | flops 8 | bytes 64 | tf_op jit(solution)/shard_map/while/body/eval_jaxpr/psum | solution.py:68
  402.8 18.2 %all-reduce.5 = (f32[4]{0:T(128)S(1)}, f32[4]{0:T(128)S(1)}) all-reduce(f32[4]{0:T(128)S(1)} %get-tuple-element.234, f32[4]{0:T(128)S(1)} %get-tuple-element.235), channel_id=1, replica_groups=mesh['gy'=8,'gx'=4] {'gy'}, use_global_device_ids=true, to_apply=%region_6.0 | all-reduce | flops 8 | bytes 64 | tf_op jit(solution)/shard_map/while/body/eval_jaxpr/psum | solution.py:68
  446.0 5.4 multiply_reduce_fusion.3
  451.4 8.1 %all-reduce.4 = (f32[4]{0:T(128)S(1)}, f32[4]{0:T(128)S(1)}) all-reduce(f32[4]{0:T(128)S(1)} %get-tuple-element.232, f32[4]{0:T(128)S(1)} %get-tuple-element.233), channel_id=1, replica_groups=mesh['gy'=8,'gx'=4] {'gx'}, use_global_device_ids=true, to_apply=%region_5.0 | all-reduce | flops 8 | bytes 64 | tf_op jit(solution)/shard_map/while/body/eval_jaxpr/psum | solution.py:68
  459.5 18.2 %all-reduce.5 = (f32[4]{0:T(128)S(1)}, f32[4]{0:T(128)S(1)}) all-reduce(f32[4]{0:T(128)S(1)} %get-tuple-element.234, f32[4]{0:T(128)S(1)} %get-tuple-element.235), channel_id=1, replica_groups=mesh['gy'=8,'gx'=4] {'gy'}, use_global_device_ids=true, to_apply=%region_6.0 | all-reduce | flops 8 | bytes 64 | tf_op jit(solution)/shard_map/while/body/eval_jaxpr/psum | solution.py:68
  508.0 8.1 %all-reduce.4 = (f32[4]{0:T(128)S(1)}, f32[4]{0:T(128)S(1)}) all-reduce(f32[4]{0:T(128)S(1)} %get-tuple-element.232, f32[4]{0:T(128)S(1)} %get-tuple-element.233), channel_id=1, replica_groups=mesh['gy'=8,'gx'=4] {'gx'}, use_global_device_ids=true, to_apply=%region_5.0 | all-reduce | flops 8 | bytes 64 | tf_op jit(solution)/shard_map/while/body/eval_jaxpr/psum | solution.py:68
  516.2 18.2 %all-reduce.5 = (f32[4]{0:T(128)S(1)}, f32[4]{0:T(128)S(1)}) all-reduce(f32[4]{0:T(128)S(1)} %get-tuple-element.234, f32[4]{0:T(128)S(1)} %get-tuple-element.235), channel_id=1, replica_groups=mesh['gy'=8,'gx'=4] {'gy'}, use_global_device_ids=true, to_apply=%region_6.0 | all-reduce | flops 8 | bytes 64 | tf_op jit(solution)/shard_map/while/body/eval_jaxpr/psum | solution.py:68
  564.7 8.1 %all-reduce.4 = (f32[4]{0:T(128)S(1)}, f32[4]{0:T(128)S(1)}) all-reduce(f32[4]{0:T(128)S(1)} %get-tuple-element.232, f32[4]{0:T(128)S(1)} %get-tuple-element.233), channel_id=1, replica_groups=mesh['gy'=8,'gx'=4] {'gx'}, use_global_device_ids=true, to_apply=%region_5.0 | all-reduce | flops 8 | bytes 64 | tf_op jit(solution)/shard_map/while/body/eval_jaxpr/psum | solution.py:68
  572.8 18.2 %all-reduce.5 = (f32[4]{0:T(128)S(1)}, f32[4]{0:T(128)S(1)}) all-reduce(f32[4]{0:T(128)S(1)} %get-tuple-element.234, f32[4]{0:T(128)S(1)} %get-tuple-element.235), channel_id=1, replica_groups=mesh['gy'=8,'gx'=4] {'gy'}, use_global_device_ids=true, to_apply=%region_6.0 | all-reduce | flops 8 | bytes 64 | tf_op jit(solution)/shard_map/while/body/eval_jaxpr/psum | solution.py:68
  621.4 8.1 %all-reduce.4 = (f32[4]{0:T(128)S(1)}, f32[4]{0:T(128)S(1)}) all-reduce(f32[4]{0:T(128)S(1)} %get-tuple-element.232, f32[4]{0:T(128)S(1)} %get-tuple-element.233), channel_id=1, replica_groups=mesh['gy'=8,'gx'=4] {'gx'}, use_global_device_ids=true, to_apply=%region_5.0 | all-reduce | flops 8 | bytes 64 | tf_op jit(solution)/shard_map/while/body/eval_jaxpr/psum | solution.py:68
  629.5 18.2 %all-reduce.5 = (f32[4]{0:T(128)S(1)}, f32[4]{0:T(128)S(1)}) all-reduce(f32[4]{0:T(128)S(1)} %get-tuple-element.234, f32[4]{0:T(128)S(1)} %get-tuple-element.235), channel_id=1, replica_groups=mesh['gy'=8,'gx'=4] {'gy'}, use_global_device_ids=true, to_apply=%region_6.0 | all-reduce | flops 8 | bytes 64 | tf_op jit(solution)/shard_map/while/body/eval_jaxpr/psum | solution.py:68
  676.9 40.7 %psum.35 = f32[4]{0:T(128)S(1)} all-reduce(f32[4]{0:T(128)S(1)} %get-tuple-element.150), channel_id=1, replica_groups=mesh['gy'=8,'gx'=4] {'gy','gx'}, use_global_device_ids=true, to_apply=%region_9.0 | all-reduce | flops 4 | bytes 32 | tf_op jit(solution)/shard_map/psum | solution.py:82
  (346 shorter events, 344.6 us)
Async XLA Ops:
  3.8 13.1 %collective-permute-start.4 = (f32[4,512]{1,0:T(4,128)S(1)}, f32[4,512]{1,0:T(4,128)S(1)}, u32[]{:S(2)}, u32[]{:S(2)}) collective-permute-start(f32[4,512]{1,0:T(4,128)S(1)} %bitcast.78), channel_id=1, source_target_pairs={{0,4},{4,8},{8,12},{12,16},{16,20},{20,24},{24,28},{1,5},{5,9},{9,... | collective-permute-start | bytes 24584 | tf_op jit(solution)/shard_map/ppermute | solution.py:14
  9.1 9.2 %collective-permute-start.5 = (f32[4,128]{1,0:T(4,128)S(1)}, f32[4,128]{1,0:T(4,128)S(1)}, u32[]{:S(2)}, u32[]{:S(2)}) collective-permute-start(f32[4,128]{1,0:T(4,128)S(1)} %slice_bitcast_fusion.2), channel_id=1, source_target_pairs={{0,1},{1,2},{2,3},{4,5},{5,6},{6,7},{8,9},{9,10},{10,11},{12,13},{... | collective-permute-start | bytes 6152 | tf_op jit(solution)/shard_map/ppermute | solution.py:14
  21.6 8.5 %collective-permute-start = (f32[4,128]{1,0:T(4,128)S(1)}, f32[4,128]{1,0:T(4,128)S(1)}, u32[]{:S(2)}, u32[]{:S(2)}) collective-permute-start(f32[4,128]{1,0:T(4,128)S(1)} %slice_bitcast_fusion.6), channel_id=1, source_target_pairs={{1,0},{2,1},{3,2},{5,4},{6,5},{7,6},{9,8},{10,9},{11,10},{13,12},{... | collective-permute-start | bytes 6152 | tf_op jit(solution)/shard_map/while/body/eval_jaxpr/ppermute | solution.py:14
  38.5 8.7 %collective-permute-start.3 = (f32[4,512]{1,0:T(4,128)S(1)}, f32[4,512]{1,0:T(4,128)S(1)}, u32[]{:S(2)}, u32[]{:S(2)}) collective-permute-start(f32[4,512]{1,0:T(4,128)S(1)} %bitcast.70), channel_id=1, source_target_pairs={{0,4},{4,8},{8,12},{12,16},{16,20},{20,24},{24,28},{1,5},{5,9},{9,... | collective-permute-start | bytes 24584 | tf_op jit(solution)/shard_map/while/body/eval_jaxpr/ppermute | solution.py:14
  42.9 5.7 collective-permute-start.2
  81.4 8.5 %collective-permute-start = (f32[4,128]{1,0:T(4,128)S(1)}, f32[4,128]{1,0:T(4,128)S(1)}, u32[]{:S(2)}, u32[]{:S(2)}) collective-permute-start(f32[4,128]{1,0:T(4,128)S(1)} %slice_bitcast_fusion.6), channel_id=1, source_target_pairs={{1,0},{2,1},{3,2},{5,4},{6,5},{7,6},{9,8},{10,9},{11,10},{13,12},{... | collective-permute-start | bytes 6152 | tf_op jit(solution)/shard_map/while/body/eval_jaxpr/ppermute | solution.py:14
  83.1 5.5 collective-permute-start.1
  98.3 6.6 collective-permute-start.3
  137.8 8.5 %collective-permute-start = (f32[4,128]{1,0:T(4,128)S(1)}, f32[4,128]{1,0:T(4,128)S(1)}, u32[]{:S(2)}, u32[]{:S(2)}) collective-permute-start(f32[4,128]{1,0:T(4,128)S(1)} %slice_bitcast_fusion.6), channel_id=1, source_target_pairs={{1,0},{2,1},{3,2},{5,4},{6,5},{7,6},{9,8},{10,9},{11,10},{13,12},{... | collective-permute-start | bytes 6152 | tf_op jit(solution)/shard_map/while/body/eval_jaxpr/ppermute | solution.py:14
  139.5 5.5 collective-permute-start.1
  154.7 6.6 collective-permute-start.3
  194.5 8.5 %collective-permute-start = (f32[4,128]{1,0:T(4,128)S(1)}, f32[4,128]{1,0:T(4,128)S(1)}, u32[]{:S(2)}, u32[]{:S(2)}) collective-permute-start(f32[4,128]{1,0:T(4,128)S(1)} %slice_bitcast_fusion.6), channel_id=1, source_target_pairs={{1,0},{2,1},{3,2},{5,4},{6,5},{7,6},{9,8},{10,9},{11,10},{13,12},{... | collective-permute-start | bytes 6152 | tf_op jit(solution)/shard_map/while/body/eval_jaxpr/ppermute | solution.py:14
  196.1 5.5 collective-permute-start.1
  211.4 6.6 collective-permute-start.3
  251.2 8.5 %collective-permute-start = (f32[4,128]{1,0:T(4,128)S(1)}, f32[4,128]{1,0:T(4,128)S(1)}, u32[]{:S(2)}, u32[]{:S(2)}) collective-permute-start(f32[4,128]{1,0:T(4,128)S(1)} %slice_bitcast_fusion.6), channel_id=1, source_target_pairs={{1,0},{2,1},{3,2},{5,4},{6,5},{7,6},{9,8},{10,9},{11,10},{13,12},{... | collective-permute-start | bytes 6152 | tf_op jit(solution)/shard_map/while/body/eval_jaxpr/ppermute | solution.py:14
  268.0 6.6 collective-permute-start.3
  307.8 8.5 %collective-permute-start = (f32[4,128]{1,0:T(4,128)S(1)}, f32[4,128]{1,0:T(4,128)S(1)}, u32[]{:S(2)}, u32[]{:S(2)}) collective-permute-start(f32[4,128]{1,0:T(4,128)S(1)} %slice_bitcast_fusion.6), channel_id=1, source_target_pairs={{1,0},{2,1},{3,2},{5,4},{6,5},{7,6},{9,8},{10,9},{11,10},{13,12},{... | collective-permute-start | bytes 6152 | tf_op jit(solution)/shard_map/while/body/eval_jaxpr/ppermute | solution.py:14
  324.7 6.6 collective-permute-start.3
  364.5 8.5 %collective-permute-start = (f32[4,128]{1,0:T(4,128)S(1)}, f32[4,128]{1,0:T(4,128)S(1)}, u32[]{:S(2)}, u32[]{:S(2)}) collective-permute-start(f32[4,128]{1,0:T(4,128)S(1)} %slice_bitcast_fusion.6), channel_id=1, source_target_pairs={{1,0},{2,1},{3,2},{5,4},{6,5},{7,6},{9,8},{10,9},{11,10},{13,12},{... | collective-permute-start | bytes 6152 | tf_op jit(solution)/shard_map/while/body/eval_jaxpr/ppermute | solution.py:14
  381.3 6.6 collective-permute-start.3
  421.1 8.5 %collective-permute-start = (f32[4,128]{1,0:T(4,128)S(1)}, f32[4,128]{1,0:T(4,128)S(1)}, u32[]{:S(2)}, u32[]{:S(2)}) collective-permute-start(f32[4,128]{1,0:T(4,128)S(1)} %slice_bitcast_fusion.6), channel_id=1, source_target_pairs={{1,0},{2,1},{3,2},{5,4},{6,5},{7,6},{9,8},{10,9},{11,10},{13,12},{... | collective-permute-start | bytes 6152 | tf_op jit(solution)/shard_map/while/body/eval_jaxpr/ppermute | solution.py:14
  438.0 6.6 collective-permute-start.3
  477.8 8.5 %collective-permute-start = (f32[4,128]{1,0:T(4,128)S(1)}, f32[4,128]{1,0:T(4,128)S(1)}, u32[]{:S(2)}, u32[]{:S(2)}) collective-permute-start(f32[4,128]{1,0:T(4,128)S(1)} %slice_bitcast_fusion.6), channel_id=1, source_target_pairs={{1,0},{2,1},{3,2},{5,4},{6,5},{7,6},{9,8},{10,9},{11,10},{13,12},{... | collective-permute-start | bytes 6152 | tf_op jit(solution)/shard_map/while/body/eval_jaxpr/ppermute | solution.py:14
  494.7 6.6 collective-permute-start.3
  534.5 8.5 %collective-permute-start = (f32[4,128]{1,0:T(4,128)S(1)}, f32[4,128]{1,0:T(4,128)S(1)}, u32[]{:S(2)}, u32[]{:S(2)}) collective-permute-start(f32[4,128]{1,0:T(4,128)S(1)} %slice_bitcast_fusion.6), channel_id=1, source_target_pairs={{1,0},{2,1},{3,2},{5,4},{6,5},{7,6},{9,8},{10,9},{11,10},{13,12},{... | collective-permute-start | bytes 6152 | tf_op jit(solution)/shard_map/while/body/eval_jaxpr/ppermute | solution.py:14
  551.3 6.6 collective-permute-start.3
  591.1 8.5 %collective-permute-start = (f32[4,128]{1,0:T(4,128)S(1)}, f32[4,128]{1,0:T(4,128)S(1)}, u32[]{:S(2)}, u32[]{:S(2)}) collective-permute-start(f32[4,128]{1,0:T(4,128)S(1)} %slice_bitcast_fusion.6), channel_id=1, source_target_pairs={{1,0},{2,1},{3,2},{5,4},{6,5},{7,6},{9,8},{10,9},{11,10},{13,12},{... | collective-permute-start | bytes 6152 | tf_op jit(solution)/shard_map/while/body/eval_jaxpr/ppermute | solution.py:14
  608.0 6.6 collective-permute-start.3
  648.1 12.8 %collective-permute-start.6 = (f32[4,512]{1,0:T(4,128)S(1)}, f32[4,512]{1,0:T(4,128)S(1)}, u32[]{:S(2)}, u32[]{:S(2)}) collective-permute-start(f32[4,512]{1,0:T(4,128)S(1)} %bitcast.77), channel_id=1, source_target_pairs={{4,0},{8,4},{12,8},{16,12},{20,16},{24,20},{28,24},{5,1},{9,5},{13... | collective-permute-start | bytes 24584 | tf_op jit(solution)/shard_map/ppermute | solution.py:14
  649.4 10.7 %collective-permute-start.7 = (f32[4,128]{1,0:T(4,128)S(1)}, f32[4,128]{1,0:T(4,128)S(1)}, u32[]{:S(2)}, u32[]{:S(2)}) collective-permute-start(f32[4,128]{1,0:T(4,128)S(1)} %slice_bitcast_fusion.3), channel_id=1, source_target_pairs={{1,0},{2,1},{3,2},{5,4},{6,5},{7,6},{9,8},{10,9},{11,10},{13,12},{... | collective-permute-start | bytes 6152 | tf_op jit(solution)/shard_map/ppermute | solution.py:14
  664.7 9.2 %collective-permute-start.9 = (f32[4,128]{1,0:T(4,128)S(1)}, f32[4,128]{1,0:T(4,128)S(1)}, u32[]{:S(2)}, u32[]{:S(2)}) collective-permute-start(f32[4,128]{1,0:T(4,128)S(1)} %slice_reduce_fusion), channel_id=1, source_target_pairs={{0,1},{1,2},{2,3},{4,5},{5,6},{6,7},{8,9},{9,10},{10,11},{12,13},{... | collective-permute-start | bytes 6152 | tf_op jit(solution)/shard_map/ppermute | solution.py:14
  667.8 6.3 collective-permute-start.8
  (34 other events, 144.1 us)
